TPU v7x, 32 devices: a whole 2x2x4 slice. The times are simulated.
32 devices in a mesh: tm: 16 (over z, x, core), chan: 2 (over y).
Axes of the slice: x: 2, y: 2, z: 4, core: 2. Of those that a mesh axis runs over, the one named last changes fastest.
Arguments:
- trans: float32 [4, 128, 32768], P(None, 'chan', 'tm'), may hold values from -1 to 1
- drive: float32 [2, 128, 32768], P(None, 'chan', 'tm'), may hold values from -60 to 60
- back_drive: float32 [2, 128, 32768], P(None, 'chan', 'tm'), may hold values from -60 to 60
- readout: float32 [128, 2, 128], P('chan'), may hold values from -0.375 to 0.375
Outputs:
- observed: float32 [128, 32768], P('chan', 'tm')
All inputs are finite; a program needn't handle non-finite values.
Results may differ from a plain program's by a relative error of at most 0.0003.
Values sent between devices are 32-bit elements; how exact they have to be, the bound alone decides.
No kernel may reach another device: no remote copies, remote signals or barrier semaphores. Data moves between devices by JAX's collectives and lax.ppermute only.
A program may use at most 64 MiB of HBM per device.

v0:
```python
import jax
import jax.numpy as jnp
from jax import lax
from jax.sharding import PartitionSpec as P

epsilon = 1e-06
identity_fill = (1.0, 0.0, 0.0, 1.0, 0.0, 0.0)


def prefix(part, axis, combine, identity, reverse):
    count = lax.axis_size(axis)
    place = lax.axis_index(axis)
    ahead = count - 1 - place if reverse else place
    gathered = jax.tree.map(lambda a: lax.all_gather(a, axis), part)
    state = jax.tree.map(lambda a, e: jnp.zeros_like(a) + jnp.asarray(e, a.dtype), part, identity)

    def one(hop, state):
        source = count - 1 - hop if reverse else hop
        return combine(
            state, jax.tree.map(lambda a: lax.dynamic_index_in_dim(a, source, 0, False), gathered)
        )

    return lax.fori_loop(0, ahead, one, state)


def compose(earlier, later):
    return (
        later[0] * earlier[0] + later[1] * earlier[2],
        later[0] * earlier[1] + later[1] * earlier[3],
        later[2] * earlier[0] + later[3] * earlier[2],
        later[2] * earlier[1] + later[3] * earlier[3],
        later[0] * earlier[4] + later[1] * earlier[5] + later[4],
        later[2] * earlier[4] + later[3] * earlier[5] + later[5],
    )


def shifted_part(array, offset, fill_value, reverse):
    filler = jnp.full((array.shape[0], offset), fill_value, array.dtype)
    if reverse:
        return jnp.concatenate([array[:, offset:], filler], axis=1)
    return jnp.concatenate([filler, array[:, :-offset]], axis=1)


def doubling_scan(pieces, reverse):
    length = pieces[0].shape[1]
    offset = 1
    while offset < length:
        shifted = tuple(
            (
                shifted_part(piece, offset, fill_value, reverse)
                for piece, fill_value in zip(pieces, identity_fill)
            )
        )
        pieces = compose(shifted, pieces)
        offset = offset * 2
    return pieces


def apply_carry(maps, carry):
    first = carry[0][:, None]
    second = carry[1][:, None]
    return (
        maps[0] * first + maps[1] * second + maps[4],
        maps[2] * first + maps[3] * second + maps[5],
    )


def on_device(trans, drive, back_drive, readout):
    channels = trans.shape[1]
    steps = trans.shape[2]
    devices_tm = lax.axis_size("tm")
    forward = doubling_scan((trans[0], trans[1], trans[2], trans[3], drive[0], drive[1]), False)
    backward = doubling_scan(
        (trans[0], trans[2], trans[1], trans[3], back_drive[0], back_drive[1]), True
    )
    ones = jnp.ones((channels,), jnp.float32)
    zeros = jnp.zeros((channels,), jnp.float32)
    identity = (ones, zeros, zeros, ones, zeros, zeros)
    before = prefix(
        (
            forward[0][:, -1],
            forward[1][:, -1],
            forward[2][:, -1],
            forward[3][:, -1],
            forward[4][:, -1],
            forward[5][:, -1],
        ),
        "tm",
        compose,
        identity,
        False,
    )
    after = prefix(
        (
            backward[0][:, 0],
            backward[1][:, 0],
            backward[2][:, 0],
            backward[3][:, 0],
            backward[4][:, 0],
            backward[5][:, 0],
        ),
        "tm",
        compose,
        identity,
        True,
    )
    forward_states = apply_carry(forward, (before[4], before[5]))
    backward_states = apply_carry(backward, (after[4], after[5]))
    sum_f, sum_b = lax.psum(
        (
            jnp.sum(
                forward_states[0] * forward_states[0] + forward_states[1] * forward_states[1],
                axis=1,
            ),
            jnp.sum(
                backward_states[0] * backward_states[0] + backward_states[1] * backward_states[1],
                axis=1,
            ),
        ),
        "tm",
    )
    count = 2.0 * steps * devices_tm
    norm_f = jnp.sqrt(sum_f / count + epsilon)[:, None]
    norm_b = jnp.sqrt(sum_b / count + epsilon)[:, None]
    smoothed = jnp.stack(
        [
            forward_states[0] / norm_f + backward_states[0] / norm_b,
            forward_states[1] / norm_f + backward_states[1] / norm_b,
        ],
        axis=0,
    )
    full_readout = lax.all_gather(readout, "chan", axis=0, tiled=True)
    mine = lax.dynamic_slice_in_dim(full_readout, lax.axis_index("chan") * channels, channels, 2)
    flat = mine.reshape(mine.shape[0], -1)
    right = smoothed.reshape(-1, steps)
    observed = lax.psum_scatter(
        jnp.dot(flat, right, precision=lax.Precision.HIGHEST, preferred_element_type=jnp.float32),
        "chan",
        scatter_dimension=0,
        tiled=True,
    )
    return observed


def solution(mesh):
    in_specs = (
        P(None, "chan", "tm"),
        P(None, "chan", "tm"),
        P(None, "chan", "tm"),
        P("chan", None, None),
    )
    out_specs = P("chan", "tm")
    return jax.shard_map(
        on_device, mesh=mesh, in_specs=in_specs, out_specs=out_specs, check_vma=False
    )
```

profile of v0, /device:TPU:0, one launch (start us, length us, event | category | flops | bytes accessed | tf_op | source)
XLA Modules:
  0.0 184.8 jit_solution(10169155482427554681)
XLA Ops:
  6.5 1.4 slice_bitcast_fusion.1
  8.6 1.1 copy-done.1
  9.7 0.3 add_add_fusion.16
  10.4 0.8 copy-done.2
  11.3 1.3 fusion.95
  12.6 1.3 fusion.97
  13.9 0.5 add_add_fusion.15
  14.9 0.5 add_add_fusion.34
  16.5 0.4 add_add_fusion.13
  17.1 0.2 multiply_add_fusion.21
  18.5 0.4 add_add_fusion.11
  19.1 0.3 multiply_add_fusion.17
  20.6 0.4 add_add_fusion.9
  21.2 0.3 multiply_add_fusion.13
  22.6 0.4 add_add_fusion.7
  23.2 0.3 multiply_add_fusion.9
  24.7 0.4 add_add_fusion.5
  25.2 0.3 multiply_add_fusion.5
  26.2 0.4 add_add_fusion.3
  26.6 0.4 multiply_add_fusion.1
  27.3 0.3 fusion.44
  28.1 0.3 fusion.60
  29.0 1.1 fusion.76
  30.1 1.0 fusion.72
  31.2 1.1 fusion.71
  32.3 1.1 fusion.78
  33.5 0.9 slice_reduce_fusion.5
  34.3 0.9 slice_reduce_fusion.4
  35.2 0.9 slice_reduce_fusion.3
  36.1 0.9 slice_reduce_fusion.2
  37.0 0.9 slice_reduce_fusion.1
  37.8 0.9 slice_reduce_fusion
  38.7 2.4 %add_add_fusion.32 = (f32[64,2048]{1,0:T(8,128)S(1)}, f32[64,2048]{1,0:T(8,128)S(1)}, f32[64,2048]{1,0:T(8,128)S(1)}, f32[64,2048]{1,0:T(8,128)S(1)}, f32[64,2048]{1,0:T(8,128)S(1)}, /*index=5*/f32[64,2048]{1,0:T(8,128)S(1)}) fusion(f32[64,2048]{1,0:T(8,128)S(1)} %get-tuple-element.505, f32[64,2046]{1,0:T(8,128)S(1)} %bitcast.215, ...), kind=kLoop, calls=%fused_computation.234 | loop fusion | flops 2621440 | bytes 9435136 | tf_op jit(solution)/shard_map/add | solution.py:33
  41.1 0.9 add_add_fusion.30
  42.0 0.9 add_add_fusion.28
  42.9 0.9 add_add_fusion.26
  43.8 0.9 add_add_fusion.24
  44.7 0.9 add_add_fusion.22
  45.7 0.9 add_add_fusion.20
  46.9 0.5 fusion.38
  47.6 0.6 fusion.54
  48.4 0.7 fusion.70
  49.2 0.3 fusion.65
  49.7 0.6 copy-done.7
  50.3 0.3 slice_reduce_fusion.10
  51.4 0.6 dynamic-slice
  52.6 0.2 dynamic-update-slice.6
  52.9 0.2 dynamic-update-slice.7
  53.1 0.2 dynamic-update-slice.8
  53.3 0.2 dynamic-update-slice.9
  53.5 0.2 dynamic-update-slice.10
  53.7 0.2 dynamic-update-slice.11
  54.1 0.2 dynamic-update-slice.1
  54.4 0.2 dynamic-update-slice.2
  54.6 0.2 dynamic-update-slice.3
  55.0 0.2 dynamic-update-slice.5
  55.2 63.1 %all-reduce.145 = (f32[1024]{0:T(1024)S(1)}, f32[1024]{0:T(1024)S(1)}, f32[1024]{0:T(1024)S(1)}, f32[1024]{0:T(1024)S(1)}, f32[1024]{0:T(1024)S(1)}, /*index=5*/...) all-reduce(f32[1024]{0:T(1024)S(1)} %dynamic-update-slice.6, ...), channel_id=8, replica_groups=mesh['tm'=16,'chan'=2] {'tm'}, use_global_device_ids=true, to_apply=%add.138 | all-reduce | flops 12288 | bytes 98304
  118.7 0.7 while.39
  119.9 2.7 %add_reduce_fusion = (f32[64]{0:T(128)S(1)}, f32[64,2048]{1,0:T(8,128)}, f32[64,2048]{1,0:T(8,128)}) fusion(f32[64,2048]{1,0:T(8,128)S(1)} %copy-done.3, f32[64,2048]{1,0:T(8,128)} %get-tuple-element.554, f32[64]{0:T(128)S(1)} %get-tuple-element.327, f32[64,2048]{1,0:T(8,128)} %get-tuple-element.553, f32[64]{0:T(128)S(1)} %get-tuple-element.326, ...), kind=kLoop, calls=%fused_computation.166 | loop fusion | flops 1572800 | bytes 4195072 | tf_op jit(solution)/shard_map/reduce_sum | solution.py:115
  122.7 0.5 add_reduce_fusion.1
  123.2 29.5 %all-reduce.144 = (f32[64]{0:T(128)S(1)}, f32[64]{0:T(128)S(1)}) all-reduce(f32[64]{0:T(128)S(1)} %get-tuple-element.385, f32[64]{0:T(128)S(1)} %get-tuple-element.382), channel_id=1, replica_groups=mesh['tm'=16,'chan'=2] {'tm'}, use_global_device_ids=true, to_apply=%region_7.8 | all-reduce | flops 128 | bytes 1024 | tf_op jit(solution)/shard_map/psum | solution.py:109
  152.7 4.9 %all_gather.39 = f32[128,2,128]{2,1,0:T(2,128)S(1)} all-gather(f32[64,2,128]{2,1,0:T(2,128)S(1)} %copy-done.17), channel_id=1, replica_groups=mesh['tm'=16,'chan'=2] {'chan'}, dimensions={0}, use_global_device_ids=true | all-gather | bytes 196608 | tf_op jit(solution)/shard_map/all_gather | solution.py:132
  158.0 2.0 %convolution_bitcast_fusion = f32[128,2048]{1,0:T(8,128)} fusion(f32[1,64,2048]{2,1,0:T(8,128)S(1)} %get-tuple-element.566, f32[1,64,2048]{2,1,0:T(8,128)S(1)} %get-tuple-element.565, f32[128,2,64]{2,1,0:T(2,128)S(1)} %constant_dynamic-slice_fusion.12), kind=kOutput, calls=%fused_computation.40 | convolution fusion | flops 402915328 | bytes 2162688 | tf_op jit(solution)/shard_map/dot_general | solution.py:137
  160.1 17.8 %reduce-scatter.2.cloned.1.call-done = f32[64,2048]{1,0:T(8,128)} async-done(((f32[128,2048]{1,0:T(8,128)}), f32[64,2048]{1,0:T(8,128)}) %reduce-scatter.2.cloned.1.call-update) | async-done | bytes 524304 | tf_op jit(solution)/shard_map/reduce_scatter | solution.py:136
  (191 shorter events, 14.0 us)
Async XLA Ops:
  6.5 1.9 %copy-start = (f32[4,64,2048]{2,1,0:T(8,128)S(1)}, f32[4,64,2048]{2,1,0:T(8,128)}, u32[]{:S(2)}) copy-start(f32[4,64,2048]{2,1,0:T(8,128)} %param.8) | copy-start | bytes 6291460
  6.5 171.4 %reduce-scatter.2.cloned.1.call-start = ((), (), s32[]{:S(2)}) async-start(), calls=%async_computation.1 | async-start | bytes 1572864 | tf_op jit(solution)/shard_map/reduce_scatter | solution.py:136
  8.4 1.2 copy-start.1
  10.0 1.2 copy-start.2
  49.2 2.2 %copy-start.18 = (u32[32]{0:T(128)S(1)}, u32[32]{0:T(128)}, u32[]{:S(2)}) copy-start(u32[32]{0:T(128)} %constant.381) | copy-start | bytes 388
  49.2 70.7 %copy-start.3 = (f32[64,2048]{1,0:T(8,128)S(1)}, f32[64,2048]{1,0:T(8,128)}, u32[]{:S(2)}) copy-start(f32[64,2048]{1,0:T(8,128)} %get-tuple-element.448) | copy-start | bytes 1572868
  49.2 70.7 %copy-start.4 = (f32[64,2048]{1,0:T(8,128)S(1)}, f32[64,2048]{1,0:T(8,128)}, u32[]{:S(2)}) copy-start(f32[64,2048]{1,0:T(8,128)} %get-tuple-element.451) | copy-start | bytes 1572868
  49.2 70.7 %copy-start.5 = (f32[64,2048]{1,0:T(8,128)S(1)}, f32[64,2048]{1,0:T(8,128)}, u32[]{:S(2)}) copy-start(f32[64,2048]{1,0:T(8,128)} %get-tuple-element.551) | copy-start | bytes 1572868
  49.2 70.7 %copy-start.6 = (f32[64,2048]{1,0:T(8,128)S(1)}, f32[64,2048]{1,0:T(8,128)}, u32[]{:S(2)}) copy-start(f32[64,2048]{1,0:T(8,128)} %get-tuple-element.552) | copy-start | bytes 1572868
  49.5 0.8 copy-start.7
  49.5 1.1 copy-start.9
  49.5 1.3 copy-start.11
  49.5 1.5 copy-start.13
  119.9 2.8 %copy-start.8 = (f32[64,2048]{1,0:T(8,128)S(1)}, f32[64,2048]{1,0:T(8,128)}, u32[]{:S(2)}) copy-start(f32[64,2048]{1,0:T(8,128)} %copy-done.7) | copy-start | bytes 1572868
  119.9 2.8 %copy-start.10 = (f32[64,2048]{1,0:T(8,128)S(1)}, f32[64,2048]{1,0:T(8,128)}, u32[]{:S(2)}) copy-start(f32[64,2048]{1,0:T(8,128)} %copy-done.9) | copy-start | bytes 1572868
  119.9 2.8 %copy-start.12 = (f32[64,2048]{1,0:T(8,128)S(1)}, f32[64,2048]{1,0:T(8,128)}, u32[]{:S(2)}) copy-start(f32[64,2048]{1,0:T(8,128)} %copy-done.11) | copy-start | bytes 1572868
  119.9 2.8 %copy-start.14 = (f32[64,2048]{1,0:T(8,128)S(1)}, f32[64,2048]{1,0:T(8,128)}, u32[]{:S(2)}) copy-start(f32[64,2048]{1,0:T(8,128)} %copy-done.13) | copy-start | bytes 1572868
  122.7 30.0 %copy-start.17 = (f32[64,2,128]{2,1,0:T(2,128)S(1)}, f32[64,2,128]{2,1,0:T(2,128)}, u32[]{:S(2)}) copy-start(f32[64,2,128]{2,1,0:T(2,128)} %param.11) | copy-start | bytes 196612
  122.7 35.2 %copy-start.15 = (f32[64,2048]{1,0:T(8,128)S(1)}, f32[64,2048]{1,0:T(8,128)}, u32[]{:S(2)}) copy-start(f32[64,2048]{1,0:T(8,128)} %get-tuple-element.386) | copy-start | bytes 1572868
  122.7 35.1 %copy-start.16 = (f32[64,2048]{1,0:T(8,128)S(1)}, f32[64,2048]{1,0:T(8,128)}, u32[]{:S(2)}) copy-start(f32[64,2048]{1,0:T(8,128)} %get-tuple-element.387) | copy-start | bytes 1572868
Sparse Core Ops, SparseCore 0:
  160.2 17.6 reduce-scatter.1
where the time goes:
time: 185 us
  blocking collectives  97.5 us (53%)
  local copies, waits for them, and re-layouts  26.6 us (14%)
  other arithmetic  25.4 us (14%)
  waiting for transfers between devices  17.8 us (10%)
  between operations  15 us (8%)
  matrix products  2.04 us (1%)
    unnamed x1, blocking collectives  63.1 us
    psum x1, blocking collectives, on_device(): lax.psum((jnp.sum(forward_states[0] * forward_states[0] + forward_states[...  29.5 us
    reduce_scatter x1, waiting for transfers between devices, on_device(): lax.psum_scatter(jnp.dot(flat, right, precision=lax.Precision.HIGHEST, pr...  17.8 us
    add x37, other arithmetic, compose(): later[2] * earlier[4] + later[3] * earlier[5] + later[5]  13.1 us
    slice x62, local copies, waits for them, and re-layouts, shifted_part(): return jnp.concatenate([array[:, offset:], filler], axis=1)  8.38 us
    unnamed x63, local copies, waits for them, and re-layouts  5.75 us
    all_gather x1, blocking collectives, on_device(): full_readout = lax.all_gather(readout, 'chan', axis=0, tiled=True)  4.93 us
    add x10, other arithmetic, compose(): later[0] * earlier[4] + later[1] * earlier[5] + later[4]  4.51 us
  transfers between devices with their start and end apart: 1, of which 1 were waited for; matrix products, arithmetic and copies ran while one was open for 0% of the time, Pallas kernels for 0%

commit v1 on v0

v1 whole, which is shorter than its diff:
```python
import jax
import jax.numpy as jnp
from jax import lax
from jax.experimental import pallas as pl
from jax.experimental.pallas import tpu as pltpu
from jax.sharding import PartitionSpec as P

epsilon = 1e-06
LANES = 128
SUBS = 8


def cmul(a, b):
    return (a[0] * b[0] - a[1] * b[1], a[0] * b[1] + a[1] * b[0])


def conj_mul(a, b):
    return (a[0] * b[0] + a[1] * b[1], a[0] * b[1] - a[1] * b[0])


def cadd(a, b):
    return (a[0] + b[0], a[1] + b[1])


def row(x, s):
    return jnp.broadcast_to(x[s : s + 1, :], (SUBS, LANES))


def scan_kernel(trans, drive, back, w, chunk, msg, raw, sems, *, channels, steps):
    portions = LANES // channels
    span = steps // portions
    length = span // SUBS
    pitch = length + 1
    piece = min(length, LANES)
    sources = (trans.at[0], trans.at[2], drive.at[0], drive.at[1], back.at[0], back.at[1])
    copies = [pltpu.make_async_copy(s, raw.at[k], sems.at[k]) for k, s in enumerate(sources)]
    for copy in copies:
        copy.start()
    for k, copy in enumerate(copies):
        copy.wait()
        for g in range(span // LANES):
            x = jnp.concatenate(
                [raw[k, :, pl.ds(q * span + g * LANES, LANES)] for q in range(portions)], axis=0
            )
            xt = x.T
            for first in range(0, LANES, piece):
                r = g * LANES + first
                w[k, pl.ds((r // length) * pitch + r % length, piece), :] = xt[first : first + piece]

    zero = jnp.zeros((SUBS, LANES), jnp.float32)
    one = jnp.ones((SUBS, LANES), jnp.float32)

    def step(i, c):
        p, f, q, g, af, bf, cf, ab, bb, cb = c
        at = lambda k, t: w[k, pl.ds(t, SUBS, stride=pitch), :]
        z = (at(0, i), at(1, i))
        p = cmul(z, p)
        f = cadd(cmul(z, f), (at(2, i), at(3, i)))
        af = af + (f[0] * f[0] + f[1] * f[1])
        bf = cadd(bf, conj_mul(p, f))
        cf = cf + (p[0] * p[0] + p[1] * p[1])
        j = length - 1 - i
        y = (at(0, j), at(1, j))
        q = conj_mul(y, q)
        g = cadd(conj_mul(y, g), (at(4, j), at(5, j)))
        ab = ab + (g[0] * g[0] + g[1] * g[1])
        bb = cadd(bb, conj_mul(q, g))
        cb = cb + (q[0] * q[0] + q[1] * q[1])
        return p, f, q, g, af, bf, cf, ab, bb, cb

    nil = (zero, zero)
    unit = (one, zero)
    p, f, q, g, af, bf, cf, ab, bb, cb = lax.fori_loop(
        0, length, step, (unit, nil, unit, nil, zero, nil, zero, zero, nil, zero), unroll=8
    )

    sub = lax.broadcasted_iota(jnp.int32, (SUBS, LANES), 0)
    portion = lax.broadcasted_iota(jnp.int32, (SUBS, LANES), 1) // channels

    def pick(mask, a, b):
        return tuple(jnp.where(mask, x, y) for x, y in zip(a, b))

    def spread(v):
        total = v
        for m in range(1, portions):
            total = total + pltpu.roll(v, m * channels, 1)
        return total

    def combine(m, v, order, edge, shift):
        start, product = nil, unit
        base_v, base_m = nil, unit
        for s in order:
            base_v = pick(sub == s, start, base_v)
            base_m = pick(sub == s, product, base_m)
            ms, vs = (row(m[0], s), row(m[1], s)), (row(v[0], s), row(v[1], s))
            start = cadd(cmul(ms, start), vs)
            product = cmul(ms, product)
        ex_v, ex_m = nil, unit
        for _ in range(portions - 1):
            nv, nm = cadd(cmul(product, ex_v), start), cmul(product, ex_m)
            nv = tuple(pltpu.roll(a, shift, 1) for a in nv)
            nm = tuple(pltpu.roll(a, shift, 1) for a in nm)
            ex_v, ex_m = pick(portion == edge, nil, nv), pick(portion == edge, unit, nm)
        base_v = cadd(base_v, cmul(base_m, ex_v))
        base_m = cmul(base_m, ex_m)
        total_v, total_m = cadd(cmul(product, ex_v), start), cmul(product, ex_m)
        last = portion == portions - 1 - edge
        total_v = tuple(spread(jnp.where(last, a, zero)) for a in total_v)
        total_m = tuple(spread(jnp.where(last, a, zero)) for a in total_m)
        return base_v, base_m, total_v, total_m

    def stats(a, b, c, v, m):
        cross = conj_mul(v, b)
        whole = a + 2.0 * cross[0] + (v[0] * v[0] + v[1] * v[1]) * c
        mixed = conj_mul(m, (b[0] + c * v[0], b[1] + c * v[1]))
        square = (m[0] * m[0] + m[1] * m[1]) * c
        return tuple(
            spread(jnp.broadcast_to(jnp.sum(x, axis=0, keepdims=True), (SUBS, LANES)))
            for x in (whole, mixed[0], mixed[1], square)
        )

    f0, p0, fe, pe = combine(p, f, range(SUBS), 0, channels)
    g0, q0, ge, _ = combine(
        q, g, range(SUBS - 1, -1, -1), portions - 1, (LANES - channels) % LANES
    )
    for k, x in enumerate(f0 + p0 + g0 + q0):
        chunk[k] = x
    rows = pe + fe + ge + stats(af, bf, cf, f0, p0) + stats(ab, bb, cb, g0, q0)
    for half in range(2):
        block = zero
        for s, x in enumerate(rows[half * SUBS : (half + 1) * SUBS]):
            block = jnp.where(sub == s, x, block)
        msg[half * SUBS : (half + 1) * SUBS, :] = block


def readout_rows(weights, s_ref, out, target, *, channels, steps):
    portions = LANES // channels
    span = steps // portions
    length = span // SUBS
    pitch = length + 1
    piece = min(length, LANES)
    left = jnp.concatenate(
        [
            jnp.concatenate(
                [pltpu.roll(weights[k], q * channels, 1) if q else weights[k] for q in range(portions)],
                axis=0,
            )
            for k in range(2)
        ],
        axis=1,
    )

    def split(x):
        high = x.astype(jnp.bfloat16)
        return high, (x - high.astype(jnp.float32)).astype(jnp.bfloat16)

    def dot(a, b):
        return lax.dot_general(a, b, (((1,), (1,)), ((), ())), preferred_element_type=jnp.float32)

    left_high, left_low = split(left)
    for g in range(span // LANES):
        parts = []
        for k in range(2):
            rows = []
            for first in range(0, LANES, piece):
                r = g * LANES + first
                rows.append(s_ref[k, pl.ds((r // length) * pitch + r % length, piece), :])
            parts.append(jnp.concatenate(rows, axis=0) if len(rows) > 1 else rows[0])
        high, low = split(jnp.concatenate(parts, axis=1))
        res = dot(left_high, high) + (dot(left_high, low) + dot(left_low, high))
        for q in range(portions):
            out[target, :, pl.ds(q * span + g * LANES, LANES)] = res[q * channels : (q + 1) * channels]


def state_kernel(place, gath, chunk, w, weights, out, s_ref, *, channels, steps, devices):
    portions = LANES // channels
    length = steps // portions // SUBS
    pitch = length + 1
    here = place[0]

    def take(j, r):
        return gath[pl.ds(j * 16 + r, 1), :]

    def full(x):
        return jnp.broadcast_to(x, (SUBS, LANES))

    def square(j, base, v):
        cross = conj_mul(v, (take(j, base + 1), take(j, base + 2)))
        return (
            take(j, base) + 2.0 * cross[0] + (v[0] * v[0] + v[1] * v[1]) * take(j, base + 3)
        )

    def walk(j, c):
        f, mine_f, sum_f, g, mine_g, sum_g = c
        sum_f = sum_f + square(j, 6, f)
        mine_f = tuple(jnp.where(j == here, a, b) for a, b in zip(f, mine_f))
        f = cadd(cmul((take(j, 0), take(j, 1)), f), (take(j, 2), take(j, 3)))
        i = devices - 1 - j
        sum_g = sum_g + square(i, 10, g)
        mine_g = tuple(jnp.where(i == here, a, b) for a, b in zip(g, mine_g))
        g = cadd(conj_mul((take(i, 0), take(i, 1)), g), (take(i, 4), take(i, 5)))
        return f, mine_f, sum_f, g, mine_g, sum_g

    last = devices - 1
    f, g = (take(0, 2), take(0, 3)), (take(last, 4), take(last, 5))
    _, f, sum_f, _, g, sum_g = lax.fori_loop(
        1, devices, walk, (f, f, take(0, 6), g, g, take(last, 10)), unroll=5
    )
    f = tuple(jnp.where(here == 0, 0.0, a) for a in f)
    g = tuple(jnp.where(here == last, 0.0, a) for a in g)
    count = 2.0 * steps * devices
    scale_f = full(1.0 / jnp.sqrt(sum_f / count + epsilon))
    scale_g = full(1.0 / jnp.sqrt(sum_g / count + epsilon))
    f, g = tuple(map(full, f)), tuple(map(full, g))
    f = cadd((chunk[0], chunk[1]), cmul((chunk[2], chunk[3]), f))
    g = cadd((chunk[4], chunk[5]), cmul((chunk[6], chunk[7]), g))
    half = length // 2

    def step(i, c, later):
        f, g = c
        at = lambda k, t: w[k, pl.ds(t, SUBS, stride=pitch), :]
        j = length - 1 - i
        f = cadd(cmul((at(0, i), at(1, i)), f), (at(2, i), at(3, i)))
        g = cadd(conj_mul((at(0, j), at(1, j)), g), (at(4, j), at(5, j)))
        for k in range(2):
            a = f[k] * scale_f
            b = g[k] * scale_g
            if later:
                a = a + s_ref[k, pl.ds(i, SUBS, stride=pitch), :]
                b = b + s_ref[k, pl.ds(j, SUBS, stride=pitch), :]
            s_ref[k, pl.ds(i, SUBS, stride=pitch), :] = a
            s_ref[k, pl.ds(j, SUBS, stride=pitch), :] = b
        return f, g

    c = lax.fori_loop(0, half, lambda i, c: step(i, c, False), (f, g), unroll=8)
    lax.fori_loop(half, length, lambda i, c: step(i, c, True), c, unroll=8)
    for t in range(weights.shape[0]):
        readout_rows(weights.at[t], s_ref, out, t, channels=channels, steps=steps)


def own_kernel(weights, s_ref, out, *, channels, steps):
    readout_rows(weights.at[0], s_ref, out, 0, channels=channels, steps=steps)


VM = pl.BlockSpec(memory_space=pltpu.VMEM)
PARAMS = pltpu.CompilerParams(vmem_limit_bytes=40 * 1024 * 1024)


def on_device(trans, drive, back_drive, readout):
    channels = trans.shape[1]
    steps = trans.shape[2]
    devices = lax.axis_size("tm")
    groups = lax.axis_size("chan")
    portions = LANES // channels
    length = steps // portions // SUBS
    rows = SUBS * (length + 1)
    rows = (rows + 7) // 8 * 8
    here = lax.axis_index("chan")
    f32 = jnp.float32

    by_part = jnp.moveaxis(readout, 1, 0)

    def weights_for(other):
        mine = lax.dynamic_slice_in_dim(by_part, other * channels, channels, 2)
        return jnp.pad(mine, ((0, 0), (0, 0), (0, LANES - channels)))

    others = []
    for k in range(1, groups):
        pairs = [(j, (j + k) % groups) for j in range(groups)]
        others.append(lax.ppermute(weights_for((here + k) % groups), "chan", pairs))

    any_spec = pl.BlockSpec(memory_space=pltpu.HBM)
    w, chunk, msg = pl.pallas_call(
        lambda *refs: scan_kernel(*refs, channels=channels, steps=steps),
        out_shape=(
            jax.ShapeDtypeStruct((6, rows, LANES), f32),
            jax.ShapeDtypeStruct((8, SUBS, LANES), f32),
            jax.ShapeDtypeStruct((16, LANES), f32),
        ),
        in_specs=[any_spec] * 3,
        out_specs=(VM, VM, VM),
        scratch_shapes=[pltpu.VMEM((6, channels, steps), f32), pltpu.SemaphoreType.DMA((6,))],
        compiler_params=PARAMS,
        name="local_scan",
    )(trans, drive, back_drive)
    gathered = lax.all_gather(msg, "tm", axis=0, tiled=True)
    place = lax.axis_index("tm").reshape(1).astype(jnp.int32)
    out, states = pl.pallas_call(
        lambda *refs: state_kernel(*refs, channels=channels, steps=steps, devices=devices),
        out_shape=(
            jax.ShapeDtypeStruct((groups - 1, channels, steps), f32),
            jax.ShapeDtypeStruct((2, rows, LANES), f32),
        ),
        in_specs=[pl.BlockSpec(memory_space=pltpu.SMEM), VM, VM, VM, VM],
        out_specs=(VM, VM),
        compiler_params=PARAMS,
        name="states",
    )(place, gathered, chunk, w, jnp.stack(others))
    received = []
    for k in range(1, groups):
        pairs = [(j, (j - k) % groups) for j in range(groups)]
        received.append(lax.ppermute(out[k - 1], "chan", pairs))
    own = pl.pallas_call(
        lambda *refs: own_kernel(*refs, channels=channels, steps=steps),
        out_shape=jax.ShapeDtypeStruct((1, channels, steps), f32),
        in_specs=[VM, VM],
        out_specs=VM,
        compiler_params=PARAMS,
        cost_estimate=pl.CostEstimate(
            flops=12 * LANES * LANES * steps, bytes_accessed=4 * channels * steps, transcendentals=0
        ),
        name="own",
    )(weights_for(here)[None], states)[0]
    for part in received:
        own = own + part
    return own


def solution(mesh):
    in_specs = (
        P(None, "chan", "tm"),
        P(None, "chan", "tm"),
        P(None, "chan", "tm"),
        P("chan", None, None),
    )
    out_specs = P("chan", "tm")
    return jax.shard_map(
        on_device, mesh=mesh, in_specs=in_specs, out_specs=out_specs, check_vma=False
    )
```

time: 185 us -> 50.1 us (0.27)
  blocking collectives: 97.5 us -> 22 us
  other arithmetic: 25.4 us -> 0.85 us
  local copies, waits for them, and re-layouts: 26.6 us -> 5.18 us
  between operations: 15 us -> 0.04 us
  Pallas kernels: 0 us -> 5.12 us
  waiting for transfers between devices: 17.8 us -> 13 us
  starting transfers between devices: 0.01 us -> 3.62 us
  matrix products: 2.04 us -> 0 us
    unnamed x1 -> x0, blocking collectives: 63.1 us -> none
    psum x1 -> x0, blocking collectives: 29.5 us -> none  [on_device(): lax.psum((jnp.sum(forward_states[0] * forward_states[0] + forward_states[...]
    add x58 -> x1, other arithmetic: 22 us -> 0.85 us  [on_device(): own = own + part]
    slice x100 -> x0, local copies, waits for them, and re-layouts: 18.1 us -> none  [the longest x62 8.38 us: shifted_part(): return jnp.concatenate([array[:, offset:], filler], axis=1)]
    reduce_scatter x1 -> x0, waiting for transfers between devices: 17.8 us -> none  [on_device(): lax.psum_scatter(jnp.dot(flat, right, precision=lax.Precision.HIGHEST, pr...]
    all_gather x1, blocking collectives: 4.93 us -> 22 us  [on_device(): gathered = lax.all_gather(msg, 'tm', axis=0, tiled=True)]
    ppermute x0 -> x2, waiting for transfers between devices: none -> 13 us  [the longest x1 13 us: on_device(): received.append(lax.ppermute(out[k - 1], 'chan', pairs))]
    pallas_call x0 -> x3, Pallas kernels: none -> 5.12 us  [the longest x1 2.84 us: on_device(): pl.pallas_call(lambda *refs: scan_kernel(*refs, channels=channels, steps=...]
  transfers between devices with their start and end apart: 1 -> 2, of which waited for: 1 -> 1; matrix products, arithmetic and copies ran while one was open for 0% -> 0% of each run, Pallas kernels for 0% -> 7%
where the time goes in v1:
time: 50.1 us; the launch traced here: 49.8 us
  blocking collectives  22 us (44%)
  waiting for transfers between devices  13 us (26%)
  local copies, waits for them, and re-layouts  5.18 us (10%)
  Pallas kernels  5.12 us (10%)
  starting transfers between devices  3.62 us (7%)
  other arithmetic  0.85 us (2%)
    all_gather x1, blocking collectives, on_device(): gathered = lax.all_gather(msg, 'tm', axis=0, tiled=True)  22 us
    ppermute x1, waiting for transfers between devices, on_device(): received.append(lax.ppermute(out[k - 1], 'chan', pairs))  13 us
    unnamed x8, local copies, waits for them, and re-layouts  4.05 us
    ppermute x1, starting transfers between devices, on_device(): others.append(lax.ppermute(weights_for((here + k) % groups), 'chan', pairs))  3.06 us
    pallas_call x1, Pallas kernels, on_device(): pl.pallas_call(lambda *refs: scan_kernel(*refs, channels=channels, steps=...  2.84 us
    pallas_call x1, Pallas kernels, on_device(): pl.pallas_call(lambda *refs: state_kernel(*refs, channels=channels, steps...  1.67 us
    another operation x1, local copies, waits for them, and re-layouts  1.11 us
  transfers between devices with their start and end apart: 2, of which 1 were waited for; matrix products, arithmetic and copies ran while one was open for 0% of the time, Pallas kernels for 7%

profile of v1, /device:TPU:0, one launch (start us, length us, event | category | flops | bytes accessed | tf_op | source)
XLA Modules:
  0.0 49.8 jit_solution(6325250942896294457)
XLA Ops:
  0.0 1.1 %constant_dynamic-slice_fusion.1 = (f32[64,2,64]{2,1,0:T(2,128)S(1)}, f32[64,2,64]{2,1,0:T(2,128)S(1)}) fusion(f32[64,2,128]{2,1,0:T(2,128)} %param.7, s32[]{:T(128)S(6)} %select_n.13, s32[]{:T(128)S(6)} %select_n.15), kind=kLoop, calls=%fused_computation.5 | loop fusion | bytes 131080 | tf_op jit(solution)/shard_map/dynamic-slice
  1.1 3.1 %collective-permute-start = (f32[2,64,128]{2,1,0:T(8,128)S(1)}, f32[2,64,128]{2,1,0:T(8,128)S(1)}, u32[]{:S(2)}, u32[]{:S(2)}) collective-permute-start(f32[2,64,128]{2,1,0:T(8,128)S(1)} %pad.8), channel_id=1, source_target_pairs={{0,1},{1,0},{2,3},{3,2},{4,5},{5,4},{6,7},{7,6},{8,9},{9,8},{10,11... | collective-permute-start | bytes 196616 | tf_op jit(solution)/shard_map/ppermute | solution.py:270
  4.2 0.0 copy-start
  4.2 1.6 %copy-done = f32[4,64,2048]{2,1,0:T(8,128)S(1)} copy-done((f32[4,64,2048]{2,1,0:T(8,128)S(1)}, f32[4,64,2048]{2,1,0:T(8,128)}, u32[]{:S(2)}) %copy-start) | copy-done | bytes 2097176
  5.8 0.0 copy-start.1
  5.8 1.2 %copy-done.1 = f32[2,64,2048]{2,1,0:T(8,128)S(1)} copy-done((f32[2,64,2048]{2,1,0:T(8,128)S(1)}, f32[2,64,2048]{2,1,0:T(8,128)}, u32[]{:S(2)}) %copy-start.1) | copy-done | bytes 1048600
  7.0 0.0 copy-start.2
  7.0 1.2 %copy-done.2 = f32[2,64,2048]{2,1,0:T(8,128)S(1)} copy-done((f32[2,64,2048]{2,1,0:T(8,128)S(1)}, f32[2,64,2048]{2,1,0:T(8,128)}, u32[]{:S(2)}) %copy-start.2) | copy-done | bytes 1048600
  8.2 2.8 %local_scan.1 = (f32[6,1032,128]{2,1,0:T(8,128)S(1)}, f32[8,8,128]{2,1,0:T(8,128)S(1)}, f32[16,128]{1,0:T(8,128)S(1)}) custom-call(f32[4,64,2048]{2,1,0:T(8,128)S(1)} %copy-done, f32[2,64,2048]{2,1,0:T(8,128)S(1)} %copy-done.1, f32[2,64,2048]{2,1,0:T(8,128)S(1)} %copy-done.2), custom_call_target="tpu_custom_call" | custom-call | tf_op jit(solution)/shard_map/local_scan/pallas_call | solution.py:273
  11.1 22.0 %all_gather.3.refs_1_ = f32[256,128]{1,0:T(8,128)S(1)} all-gather(f32[16,128]{1,0:T(8,128)S(1)} %get-tuple-element.10), channel_id=1, replica_groups=mesh['tm'=16,'chan'=2] {'tm'}, dimensions={0}, use_global_device_ids=true | all-gather | bytes 139264 | tf_op jit(solution)/shard_map/all_gather | solution.py:286
  33.1 0.0 collective-permute-done
  33.1 1.7 %states.1 = (f32[1,64,2048]{2,1,0:T(8,128)S(1)}, f32[2,1032,128]{2,1,0:T(8,128)S(1)}) custom-call(s32[1]{0:T(128)} %bitcast.2.refs_0_, f32[256,128]{1,0:T(8,128)S(1)} %all_gather.3.refs_1_, f32[8,8,128]{2,1,0:T(8,128)S(1)} %get-tuple-element.11.refs_2_, f32[6,1032,128]{2,1,0:T(8,128)S(1)} %get-tuple-element.12.refs_3_, f32[1,2,64,128]{3,2,1,0:T(8,128)S(1)} %bitcast.13), custom_call_target="tpu_custom_call" | custom-call | tf_op jit(solution)/shard_map/states/pallas_call | solution.py:288
  34.7 0.6 %collective-permute-start.1 = (f32[64,2048]{1,0:T(8,128)S(1)}, f32[64,2048]{1,0:T(8,128)S(1)}, u32[]{:S(2)}, u32[]{:S(2)}) collective-permute-start(f32[64,2048]{1,0:T(8,128)S(1)} %bitcast.14), channel_id=1, source_target_pairs={{0,1},{1,0},{2,3},{3,2},{4,5},{5,4},{6,7},{7,6},{8,9},{9,8},{10,11... | collective-permute-start | bytes 1572872 | tf_op jit(solution)/shard_map/ppermute | solution.py:302
  35.3 0.6 %own.1 = f32[1,64,2048]{2,1,0:T(8,128)S(1)} custom-call(f32[1,2,64,128]{3,2,1,0:T(8,128)S(1)} %pad_bitcast_fusion.refs_0_, f32[2,1032,128]{2,1,0:T(8,128)S(1)} %get-tuple-element.13.refs_1_), custom_call_target="tpu_custom_call" | custom-call | flops 402653184 | bytes 524288 | tf_op jit(solution)/shard_map/own/pallas_call | solution.py:303
  35.9 13.0 %collective-permute-done.1 = f32[64,2048]{1,0:T(8,128)S(1)} collective-permute-done((f32[64,2048]{1,0:T(8,128)S(1)}, f32[64,2048]{1,0:T(8,128)S(1)}, u32[]{:S(2)}, u32[]{:S(2)}) %collective-permute-start.1) | collective-permute-done | bytes 524320 | tf_op jit(solution)/shard_map/ppermute | solution.py:302
  49.0 0.8 %bitcast_add_fusion = f32[64,2048]{1,0:T(8,128)} fusion(f32[64,2048]{1,0:T(8,128)S(1)} %collective-permute-done.1, f32[1,64,2048]{2,1,0:T(8,128)S(1)} %own.1), kind=kLoop, calls=%fused_computation | loop fusion | flops 131072 | bytes 1572864 | tf_op jit(solution)/shard_map/add | solution.py:315
  (4 shorter events, 0.0 us)
Async XLA Ops:
  1.1 31.9 %collective-permute-start = (f32[2,64,128]{2,1,0:T(8,128)S(1)}, f32[2,64,128]{2,1,0:T(8,128)S(1)}, u32[]{:S(2)}, u32[]{:S(2)}) collective-permute-start(f32[2,64,128]{2,1,0:T(8,128)S(1)} %pad.8), channel_id=1, source_target_pairs={{0,1},{1,0},{2,3},{3,2},{4,5},{5,4},{6,7},{7,6},{8,9},{9,8},{10,11... | collective-permute-start | bytes 196616 | tf_op jit(solution)/shard_map/ppermute | solution.py:270
  4.2 1.6 %copy-start = (f32[4,64,2048]{2,1,0:T(8,128)S(1)}, f32[4,64,2048]{2,1,0:T(8,128)}, u32[]{:S(2)}) copy-start(f32[4,64,2048]{2,1,0:T(8,128)} %refs_0_.1) | copy-start | bytes 6291460
  5.8 1.2 %copy-start.1 = (f32[2,64,2048]{2,1,0:T(8,128)S(1)}, f32[2,64,2048]{2,1,0:T(8,128)}, u32[]{:S(2)}) copy-start(f32[2,64,2048]{2,1,0:T(8,128)} %refs_1_.1) | copy-start | bytes 3145732
  7.0 1.2 %copy-start.2 = (f32[2,64,2048]{2,1,0:T(8,128)S(1)}, f32[2,64,2048]{2,1,0:T(8,128)}, u32[]{:S(2)}) copy-start(f32[2,64,2048]{2,1,0:T(8,128)} %refs_2_.1) | copy-start | bytes 3145732
  34.7 14.2 %collective-permute-start.1 = (f32[64,2048]{1,0:T(8,128)S(1)}, f32[64,2048]{1,0:T(8,128)S(1)}, u32[]{:S(2)}, u32[]{:S(2)}) collective-permute-start(f32[64,2048]{1,0:T(8,128)S(1)} %bitcast.14), channel_id=1, source_target_pairs={{0,1},{1,0},{2,3},{3,2},{4,5},{5,4},{6,7},{7,6},{8,9},{9,8},{10,11... | collective-permute-start | bytes 1572872 | tf_op jit(solution)/shard_map/ppermute | solution.py:302
